TPU v7x, 32 devices: a whole 2x2x4 slice. The times are simulated.
32 devices in a mesh: gx: 16 (over z, y, x), gz: 2 (over core).
Axes of the slice: x: 2, y: 2, z: 4, core: 2. Of those that a mesh axis runs over, the one named last changes fastest.
Arguments:
- flow: float32 [4, 16, 512, 128], P(None, 'gz', 'gx'), may hold values from -6 to 6
- fluid: float32 [16, 512, 128], P('gz', 'gx'), may hold values from 0.2 to 5
- density: float32 [16, 512, 128], P('gz', 'gx'), may hold values from 0.35 to 0.92
- thickness: float32 [512, 128], P('gx'), may hold values from 0.5 to 4
- bed: float32 [512, 128], P('gx'), may hold values from -6 to 6
- smb: float32 [512, 128], P('gx'), may hold values from -3 to 3
- mask: int32 [512, 128], P('gx'), may hold values from 0 to 2
Outputs:
- flow_out: float32 [4, 16, 512, 128], P(None, 'gz', 'gx')
- new_thickness: float32 [512, 128], P('gx')
- overburden: float32 [16, 512, 128], P('gz', 'gx')
Inputs may be any that keep to these rules, and one draw needn't show every extreme that they name: `mask`: 0 marks an ice-free column, 1 grounded ice, 2 floating ice.
All inputs are finite; a program needn't handle non-finite values.
Results may differ from a plain program's by a relative error of at most 0.00002.
Values sent between devices are 32-bit elements; how exact they have to be, the bound alone decides.
A program may use at most 64 MiB of HBM per device.

v0:
```python
import functools

import jax
import jax.numpy as jnp
from jax import lax
from jax.experimental import pallas as pl
from jax.experimental.pallas import tpu as pltpu
from jax.sharding import PartitionSpec as P

REGULAR = 0.01
FRICTION = 2.0
STEP = 0.2
TIME_STEP = 0.5

XH = 5
ZH = 4
PAD = 16
MESH = pl.DeviceIdType.MESH


def kernel(nx, nz, nl, nxl, flow, fluid, density, thickness, bed, smb, mask,
           flow_out, new_thickness, overburden,
           S0, S1, T, V, G, M, SM, DN, A, FX, FS, FR,
           loc, send, recv, fsend, frecv):
    gx, gz = lax.axis_index("gx"), lax.axis_index("gz")
    left, right = lax.rem(gx + nx - 1, nx), lax.rem(gx + 1, nx)
    down, up = lax.rem(gz + nz - 1, nz), lax.rem(gz + 1, nz)
    has_left, has_right = gx > 0, gx < nx - 1
    has_down, has_up = gz > 0, gz < nz - 1
    ny = flow.shape[-1]
    levels_total = nl * nz
    depth, rows = S0.shape[1], S0.shape[2]
    if nz == 2:
        base = 1 + ZH * gz
        base_up, base_down = 1 + ZH, 1

        def span(h):
            return base - h * gz, nl + h
    else:
        base = base_up = base_down = 1 + ZH

        def span(h):
            return base - h, nl + 2 * h

    own = pl.ds(base, nl)
    mine = slice(PAD, PAD + nxl)
    lo, hi = PAD - 8, PAD + nxl + 8
    c, m, p = slice(lo, hi), slice(lo - 1, hi - 1), slice(lo + 1, hi + 1)
    width = hi - lo

    copies = [
        pltpu.make_async_copy(flow, S0.at[pl.ds(0, 4), own, mine], loc.at[0]),
        pltpu.make_async_copy(fluid, S0.at[4, own, mine], loc.at[1]),
        pltpu.make_async_copy(thickness, G.at[0, mine], loc.at[2]),
        pltpu.make_async_copy(bed, G.at[1, mine], loc.at[3]),
        pltpu.make_async_copy(mask, M.at[mine], loc.at[4]),
        pltpu.make_async_copy(density, DN, loc.at[5]),
        pltpu.make_async_copy(smb, SM, loc.at[6]),
    ]
    for copy in copies:
        copy.start()

    barrier = pltpu.get_barrier_semaphore()

    @pl.when(has_left)
    def _():
        pl.semaphore_signal(barrier, inc=1, device_id={"gx": left}, device_id_type=MESH)

    @pl.when(has_right)
    def _():
        pl.semaphore_signal(barrier, inc=1, device_id={"gx": right}, device_id_type=MESH)

    for off in range(1, nz):
        pl.semaphore_signal(barrier, inc=1, device_id={"gz": lax.rem(gz + off, nz)}, device_id_type=MESH)

    zrow = jnp.zeros((rows, ny), jnp.float32)
    for k in (0, depth - 1):
        for f in range(4):
            S0[f, k] = zrow
            S1[f, k] = zrow
        for f in range(3):
            T[f, k] = zrow

    def outside_x(where):
        strip = slice(PAD - 8, PAD) if where == 0 else slice(PAD + nxl, PAD + nxl + 8)
        zero = jnp.zeros((8, ny), jnp.float32)

        def one(k, _):
            for f in range(4):
                S0[f, k, strip] = zero
            S0[4, k, strip] = zero + 1.0
            return 0

        lax.fori_loop(1, depth - 1, one, 0)
        G[0, strip] = zero
        G[1, strip] = zero
        M[strip] = jnp.zeros((8, ny), jnp.int32)

    @pl.when(jnp.logical_not(has_left))
    def _():
        outside_x(0)

    @pl.when(jnp.logical_not(has_right))
    def _():
        outside_x(1)

    if nz > 2:
        def outside_z(start):
            for k in range(start, start + ZH):
                for f in range(4):
                    S0[f, k, c] = jnp.zeros((width, ny), jnp.float32)
                S0[4, k, c] = jnp.ones((width, ny), jnp.float32)

        @pl.when(jnp.logical_not(has_down))
        def _():
            outside_z(1)

        @pl.when(jnp.logical_not(has_up))
        def _():
            outside_z(1 + ZH + nl)

    def remote(src, dst, number, device):
        return pltpu.make_async_remote_copy(src_ref=src, dst_ref=dst, send_sem=send.at[number],
                                            recv_sem=recv.at[number], device_id=device, device_id_type=MESH)

    first, last = pl.ds(PAD, XH), pl.ds(PAD + nxl - XH, XH)
    from_left, from_right = pl.ds(PAD - XH, XH), pl.ds(PAD + nxl, XH)
    every = pl.ds(0, 5)
    leftward = [
        remote(S0.at[every, own, first], S0.at[every, own, from_right], 0, {"gx": left}),
        remote(G.at[:, first], G.at[:, from_right], 1, {"gx": left}),
        remote(M.at[first], M.at[from_right], 2, {"gx": left}),
    ]
    rightward = [
        remote(S0.at[every, own, last], S0.at[every, own, from_left], 3, {"gx": right}),
        remote(G.at[:, last], G.at[:, from_left], 4, {"gx": right}),
        remote(M.at[last], M.at[from_left], 5, {"gx": right}),
    ]
    top, bottom = pl.ds(base + nl - ZH, ZH), pl.ds(base, ZH)
    from_down, from_up = pl.ds(base_up - ZH, ZH), pl.ds(base_down + nl, ZH)
    pieces = (pl.ds(PAD, nxl), from_left, from_right)
    upward = [remote(S0.at[every, top, piece], S0.at[every, from_down, piece], 6 + n, {"gz": up})
              for n, piece in enumerate(pieces)]
    downward = [remote(S0.at[every, bottom, piece], S0.at[every, from_up, piece], 9 + n, {"gz": down})
                for n, piece in enumerate(pieces)]

    for n in range(5):
        copies[n].wait()
    pl.semaphore_wait(barrier, nz - 1 + jnp.where(has_left, 1, 0) + jnp.where(has_right, 1, 0))

    @pl.when(has_left)
    def _():
        for copy in leftward:
            copy.start()

    @pl.when(has_right)
    def _():
        for copy in rightward:
            copy.start()

    @pl.when(has_up)
    def _():
        upward[0].start()

    @pl.when(has_down)
    def _():
        downward[0].start()

    copies[5].wait()
    copies[6].wait()
    total = jnp.zeros((nxl, ny), jnp.float32)
    for k in reversed(range(nl)):
        cell = DN[k]
        DN[k] = total + 0.5 * cell
        total = total + cell
    FS[2, mine] = total

    def dy(f):
        axis = f.ndim - 1
        lane = lax.broadcasted_iota(jnp.int32, f.shape, axis)
        return (jnp.where(lane < ny - 1, pltpu.roll(f, ny - 1, axis), 0.0)
                - jnp.where(lane > 0, pltpu.roll(f, 1, axis), 0.0))

    def inside(start, height):
        column = gx * nxl + lax.broadcasted_iota(jnp.int32, (height, ny), 0) + (start - PAD)
        return (column >= 0) & (column < nx * nxl)

    def plan(start, height):
        c = slice(start, start + height)
        A[0, c] = 0.5 * (FX[start + 1:start + height + 1] - FX[start - 1:start + height - 1])
        A[1, c] = 0.5 * dy(FX[c])
        A[2, c] = jnp.where(inside(start, height) & (M[c] > 0), 1.0, 0.0)
        A[3, c] = jnp.where(M[c] == 1, FRICTION, 0.0)

    def level_at(k, count):
        return gz * nl + k - base + lax.broadcasted_iota(jnp.int32, (count, 1, ny), 0)

    def stress(B, k, count, start, height):
        at = pl.ds(k, count)
        c = slice(start, start + height)
        m, p = slice(start - 1, start + height - 1), slice(start + 1, start + height + 1)
        above, below = pl.ds(k + 1, count), pl.ds(k - 1, count)
        xx, vx, wx = (B[f, at, p] - B[f, at, m] for f in range(3))
        uz, vz, zz = (B[f, above, c] - B[f, below, c] for f in range(3))
        uy, yy, wy = (dy(B[f, at, c]) for f in range(3))
        xy, xz, yz = uy + vx, uz + wx, vz + wy
        twice = xx * xx + yy * yy + zz * zz
        second = 0.0625 * (twice + twice + (xy * xy + xz * xz + yz * yz))
        third = jnp.log2(S0[4, at, c] * (second + REGULAR)) * (1.0 / 3.0)
        a = jnp.exp2(-third)
        V[0, at, c] = (2.0 * STEP) * jnp.exp2(third)
        V[1, at, c] = (0.25 * STEP) * a * (xx + yy + zz)
        h = 0.25 * a
        if height == 8:
            h = jnp.where(jnp.broadcast_to(inside(start, height)[None], h.shape), h, 0.0)
        if nz > 2:
            level = level_at(k, count)
            ok = jnp.where((level >= 0) & (level < levels_total), 1.0, 0.0)
            h = jnp.where(jnp.broadcast_to(ok, h.shape) > 0.0, h, 0.0)
        g = 0.5 * h
        T[0, at, c] = g * xz
        T[1, at, c] = g * yz
        T[2, at, c] = h * zz
        T[3, at, c] = h * xx
        T[4, at, c] = g * xy
        T[5, at, c] = h * yy

    def move(B, k, count, start, height):
        at = pl.ds(k, count)
        c = slice(start, start + height)
        m, p = slice(start - 1, start + height - 1), slice(start + 1, start + height + 1)
        above, below = pl.ds(k + 1, count), pl.ds(k - 1, count)
        level = level_at(k, count)
        drag = jnp.where(level == 0, 1.0, 0.0) * A[3, c][None]
        u, v, press = B[0, at, c], B[1, at, c], B[3, at, c]
        fx = ((T[3, at, p] - T[3, at, m]) + dy(T[4, at, c]) + (T[0, above, c] - T[0, below, c])
              - 0.5 * (B[3, at, p] - B[3, at, m]) - A[0, c][None] - drag * u)
        fy = ((T[4, at, p] - T[4, at, m]) + dy(T[5, at, c]) + (T[1, above, c] - T[1, below, c])
              - 0.5 * dy(press) - A[1, c][None] - drag * v)
        fz = ((T[0, at, p] - T[0, at, m]) + dy(T[1, at, c]) + (T[2, above, c] - T[2, below, c])
              - 0.5 * (B[3, above, c] - B[3, below, c]))
        step = V[0, at, c]
        ice = jnp.broadcast_to(A[2, c][None], u.shape)
        if nz > 2:
            ice = ice * jnp.where((level >= 0) & (level < levels_total), 1.0, 0.0)
        return [jnp.where(ice > 0.0, value, 0.0) for value in (
            u + step * fx, v + step * fy, B[2, at, c] + step * fz, press - V[1, at, c])]

    def blocks(reach, most, step, areas):
        start, count = span(reach)
        pieces = -(-count // most)
        for n in range(pieces):
            one, two = count * n // pieces, count * (n + 1) // pieces
            for area in areas:
                step(start + one, two - one, *area)

    def stress_first(*at):
        stress(S0, *at)

    def stress_last(*at):
        stress(S1, *at)

    def move_first(k, count, start, height):
        for f, value in enumerate(move(S0, k, count, start, height)):
            S1[f, pl.ds(k, count), start:start + height] = value

    def move_last(k, count, start, height):
        for f, value in enumerate(move(S1, k, count, start, height)):
            flow_out[f, pl.ds(k - base, count), start:start + height] = value

    middle = [(PAD + 1, nxl - 2)]
    FX[mine] = G[1, mine] + G[0, mine]
    plan(*middle[0])
    for flag, group in ((has_down, upward), (has_up, downward)):
        @pl.when(flag)
        def _():
            group[0].wait_recv()

    blocks(3, 2, stress_first, middle)
    blocks(2, 2, move_first, middle)
    blocks(1, 2, stress_last, middle)

    @pl.when(has_left)
    def _():
        for copy in rightward:
            copy.wait_recv()

    @pl.when(has_left & has_up)
    def _():
        upward[1].start()

    @pl.when(has_left & has_down)
    def _():
        downward[1].start()

    @pl.when(has_right)
    def _():
        for copy in leftward:
            copy.wait_recv()

    @pl.when(has_right & has_up)
    def _():
        upward[2].start()

    @pl.when(has_right & has_down)
    def _():
        downward[2].start()

    blocks(0, 2, move_last, middle)

    ends = [(PAD - 4, 8), (PAD + nxl - 4, 8)]
    for start in (PAD - 8, PAD + nxl):
        strip = slice(start, start + 8)
        FX[strip] = G[1, strip] + G[0, strip]
    for area in ends:
        plan(*area)
    for flag, group in ((has_down, upward), (has_up, downward)):
        @pl.when(flag & has_left)
        def _():
            group[1].wait_recv()

        @pl.when(flag & has_right)
        def _():
            group[2].wait_recv()

    blocks(3, 6, stress_first, ends)
    blocks(2, 6, move_first, [(PAD - 5, 8), (PAD + nxl - 3, 8)])
    blocks(1, 6, stress_last, ends)
    blocks(0, 4, move_last, ends)
    sum_u, sum_v = flow_out[0, 0, c], flow_out[1, 0, c]
    for k in range(1, nl):
        sum_u = sum_u + flow_out[0, k, c]
        sum_v = sum_v + flow_out[1, k, c]
    FS[0, c] = sum_u
    FS[1, c] = sum_v

    sums = [pltpu.make_async_remote_copy(
        src_ref=FS.at[:, pl.ds(lo, width)], dst_ref=FR.at[off - 1, :, pl.ds(lo, width)],
        send_sem=fsend.at[off - 1], recv_sem=frecv.at[off - 1],
        device_id={"gz": lax.rem(gz + off, nz)}, device_id_type=MESH) for off in range(1, nz)]
    for copy in sums:
        copy.start()
    above = jnp.zeros((nxl, ny), jnp.float32)
    for off in range(1, nz):
        sums[off - 1].wait_recv()
        sum_u = sum_u + FR[off - 1, 0, c]
        sum_v = sum_v + FR[off - 1, 1, c]
        above = above + jnp.where(gz < off, 1.0, 0.0) * FR[off - 1, 2, mine]
    part = G[0, c] * (1.0 / levels_total)
    FX[c] = part * sum_u
    flux_y = dy(part * sum_v)[8:8 + nxl]
    spread = FX[PAD + 1:PAD + nxl + 1] - FX[PAD - 1:PAD + nxl - 1] + flux_y
    fresh = G[0, mine] + TIME_STEP * (SM[...] - 0.5 * spread)
    new_thickness[...] = fresh
    weight = fresh * (1.0 / levels_total)
    for k in range(nl):
        overburden[k] = weight * (above + DN[k])

    @pl.when(has_left)
    def _():
        for copy in leftward:
            copy.wait_send()

    @pl.when(has_right)
    def _():
        for copy in rightward:
            copy.wait_send()

    for flag, group in ((has_up, upward), (has_down, downward)):
        @pl.when(flag)
        def _():
            group[0].wait_send()

        @pl.when(flag & has_left)
        def _():
            group[1].wait_send()

        @pl.when(flag & has_right)
        def _():
            group[2].wait_send()

    for copy in sums:
        copy.wait_send()


def write(nxl, held, fresh, weight, flow_out, new_thickness, overburden, done):
    copies = [
        pltpu.make_async_copy(held.at[:, :, pl.ds(PAD, nxl)], flow_out, done.at[0]),
        pltpu.make_async_copy(fresh, new_thickness, done.at[1]),
        pltpu.make_async_copy(weight, overburden, done.at[2]),
    ]
    for copy in copies:
        copy.start()
    for copy in copies:
        copy.wait()


def solution(mesh):
    nx, nz = mesh.shape["gx"], mesh.shape["gz"]

    def body(flow, fluid, density, thickness, bed, smb, mask):
        nl, nxl, ny = fluid.shape
        depth = nl + 2 + (ZH if nz == 2 else 2 * ZH)
        rows = nxl + 2 * PAD
        f32 = jnp.float32
        vmem = pl.BlockSpec(memory_space=pltpu.VMEM)
        held, fresh, weight = pl.pallas_call(
            functools.partial(kernel, nx, nz, nl, nxl),
            out_shape=(
                pltpu.VMEM((4, nl, rows, ny), f32),
                pltpu.VMEM(thickness.shape, f32),
                pltpu.VMEM(density.shape, f32),
            ),
            in_specs=[pl.BlockSpec(memory_space=pl.ANY)] * 7,
            out_specs=(vmem, vmem, vmem),
            scratch_shapes=[
                pltpu.VMEM((5, depth, rows, ny), f32),
                pltpu.VMEM((4, depth, rows, ny), f32),
                pltpu.VMEM((6, depth, rows, ny), f32),
                pltpu.VMEM((2, depth, rows, ny), f32),
                pltpu.VMEM((2, rows, ny), f32),
                pltpu.VMEM((rows, ny), jnp.int32),
                pltpu.VMEM((nxl, ny), f32),
                pltpu.VMEM((nl, nxl, ny), f32),
                pltpu.VMEM((4, rows, ny), f32),
                pltpu.VMEM((rows, ny), f32),
                pltpu.VMEM((3, rows, ny), f32),
                pltpu.VMEM((nz - 1, 3, rows, ny), f32),
                pltpu.SemaphoreType.DMA((7,)),
                pltpu.SemaphoreType.DMA((12,)),
                pltpu.SemaphoreType.DMA((12,)),
                pltpu.SemaphoreType.DMA((nz - 1,)),
                pltpu.SemaphoreType.DMA((nz - 1,)),
            ],
            compiler_params=pltpu.CompilerParams(collective_id=0, has_side_effects=True),
        )(flow, fluid, density, thickness, bed, smb, mask)
        anywhere = pl.BlockSpec(memory_space=pl.ANY)
        return pl.pallas_call(
            functools.partial(write, nxl),
            out_shape=(
                jax.ShapeDtypeStruct(flow.shape, f32),
                jax.ShapeDtypeStruct(thickness.shape, f32),
                jax.ShapeDtypeStruct(density.shape, f32),
            ),
            in_specs=[vmem] * 3,
            out_specs=(anywhere,) * 3,
            scratch_shapes=[pltpu.SemaphoreType.DMA((3,))],
        )(*(pltpu.with_memory_space_constraint(x, pltpu.VMEM) for x in (held, fresh, weight)))

    placed = (
        P(None, "gz", "gx", None), P("gz", "gx", None), P("gz", "gx", None),
        P("gx", None), P("gx", None), P("gx", None), P("gx", None),
    )
    return jax.shard_map(
        body, mesh=mesh, in_specs=placed,
        out_specs=(P(None, "gz", "gx", None), P("gx", None), P("gz", "gx", None)),
        check_vma=False,
    )
```

profile of v0, /device:TPU:29, one launch (start us, length us, event | category | flops | bytes accessed | tf_op | source)
XLA Modules:
  0.0 13.5 jit_solution(6312429020358241200)
XLA Ops:
  0.6 11.9 %shard_map.94 = (f32[4,8,64,128]{3,2,1,0:T(8,128)S(1)}, f32[32,128]{1,0:T(8,128)S(1)}, f32[8,32,128]{2,1,0:T(8,128)S(1)}) custom-call(f32[4,8,32,128]{3,2,1,0:T(8,128)} %flow.1, f32[8,32,128]{2,1,0:T(8,128)} %fluid.1, f32[8,32,128]{2,1,0:T(8,128)} %density.1, f32[32,128]{1,0:T(8,128)} %thickness.1, f32[32,128]{1,0:T(8,128)} %bed.1, f32[32,128]{1,0:T(8,128)} %smb.1, ...), custom_call_target="tpu_custom_call" | custom-call | tf_op jit(solution)/shard_map/pallas_call | solution.py:407
  12.6 0.9 %shard_map.95 = (f32[4,8,32,128]{3,2,1,0:T(8,128)}, f32[32,128]{1,0:T(8,128)}, f32[8,32,128]{2,1,0:T(8,128)}) custom-call(f32[4,8,64,128]{3,2,1,0:T(8,128)S(1)} %get-tuple-element.6.held, f32[32,128]{1,0:T(8,128)S(1)} %get-tuple-element.7.fresh, f32[8,32,128]{2,1,0:T(8,128)S(1)} %get-tuple-element.8.weight), custom_call_target="tpu_custom_call" | custom-call | tf_op jit(solution)/shard_map/pallas_call | solution.py:438
where the time goes:
time: 13.6 us; the launch traced here: 13.5 us
  Pallas kernels  12.8 us (94%)
  between operations  0.64 us (5%)
    pallas_call x1, Pallas kernels, body(): pl.pallas_call(functools.partial(kernel, nx, nz, nl, nxl), out_shape=(plt...  11.9 us
    pallas_call x1, Pallas kernels, body(): pl.pallas_call(functools.partial(write, nxl), out_shape=(jax.ShapeDtypeSt...  0.86 us

commit v1 on v0

--- a/solution.py
+++ b/solution.py
@@ -383,6 +383,877 @@
         copy.wait_send()
 
 
+def paired(nx, nl, nxl, flow, fluid, density, thickness, bed, smb, mask,
+           flow_out, new_thickness, overburden,
+           S0, S1, T, V, G, M, PK, RK, SM, DN, A, FX, FM, RM, FE, RE, FD, RD,
+           loc, ready, send, recv):
+    gx, gz = lax.axis_index("gx"), lax.axis_index("gz")
+    left, right = lax.rem(gx + nx - 1, nx), lax.rem(gx + 1, nx)
+    has_left, has_right = gx > 0, gx < nx - 1
+    odd = lax.rem(gx, 2)
+    near = gx + 1 - 2 * odd
+    far = lax.rem(gx + nx - 1 + 2 * odd, nx)
+    has_far = jnp.where(odd == 1, gx, nx - 1 - gx) < nx - 1
+    ny = flow.shape[-1]
+    levels_total = 2 * nl
+    depth, rows = S0.shape[1], S0.shape[2]
+    base = 1 + ZH * gz
+    own = pl.ds(base, nl)
+    facing = pl.ds(1 + nl - ZH + gz * (2 * ZH - nl), ZH)
+    others = pl.ds(1 + gz * 2 * ZH, nl - ZH)
+    across = pl.ds(1 + gz * nl, ZH)
+    mine = slice(PAD, PAD + nxl)
+
+    barrier = pltpu.get_barrier_semaphore()
+    pl.semaphore_signal(barrier, inc=1, device_id={"gx": near, "gz": 0}, device_id_type=MESH)
+
+    @pl.when(has_far)
+    def _():
+        pl.semaphore_signal(barrier, inc=1, device_id={"gx": far, "gz": 1}, device_id_type=MESH)
+
+    @pl.when(gz == 1)
+    def _():
+        pl.semaphore_signal(barrier, inc=1, device_id={"gz": 0}, device_id_type=MESH)
+
+    copies = [
+        pltpu.make_async_copy(flow, S0.at[pl.ds(0, 4), own, mine], loc.at[0]),
+        pltpu.make_async_copy(fluid, S0.at[4, own, mine], loc.at[1]),
+        pltpu.make_async_copy(thickness, G.at[0, mine], loc.at[2]),
+        pltpu.make_async_copy(bed, G.at[1, mine], loc.at[3]),
+        pltpu.make_async_copy(mask, M, loc.at[4]),
+        pltpu.make_async_copy(density, DN, loc.at[5]),
+        pltpu.make_async_copy(smb, SM, loc.at[6]),
+    ]
+    for copy in copies:
+        copy.start()
+
+    zrow = jnp.zeros((rows, ny), jnp.float32)
+    for k in (0, depth - 1):
+        for f in range(4):
+            S0[f, k] = zrow
+            S1[f, k] = zrow
+        for f in range(3):
+            T[f, k] = zrow
+
+    def outside_x(where):
+        strip = slice(PAD - 8, PAD) if where == 0 else slice(PAD + nxl, PAD + nxl + 8)
+        zero = jnp.zeros((8, ny), jnp.float32)
+
+        def one(k, _):
+            for f in range(4):
+                S0[f, k, strip] = zero
+            S0[4, k, strip] = zero + 1.0
+            return 0
+
+        lax.fori_loop(1, depth - 1, one, 0)
+        G[0, strip] = zero
+        G[2, strip] = zero
+        FX[strip] = zero
+
+    @pl.when(jnp.logical_not(has_left))
+    def _():
+        outside_x(0)
+
+    @pl.when(jnp.logical_not(has_right))
+    def _():
+        outside_x(1)
+
+    def remote(src, dst, number, device):
+        return pltpu.make_async_remote_copy(src_ref=src, dst_ref=dst, send_sem=send.at[number],
+                                            recv_sem=recv.at[number], device_id=device, device_id_type=MESH)
+
+    motion, state = pl.ds(0, 3), pl.ds(3, 2)
+
+    def halo(levels, src, dst, number, device):
+        (src_uvw, src_pf), (dst_uvw, dst_pf) = src, dst
+        return [remote(S0.at[motion, levels, src_uvw], S0.at[motion, levels, dst_uvw], number, device),
+                remote(S0.at[state, levels, src_pf], S0.at[state, levels, dst_pf], number + 1, device)]
+
+    first = pl.ds(PAD, XH), pl.ds(PAD, XH - 1)
+    last = pl.ds(PAD + nxl - XH, XH), pl.ds(PAD + nxl - XH + 1, XH - 1)
+    from_left = pl.ds(PAD - XH, XH), pl.ds(PAD - XH + 1, XH - 1)
+    from_right = pl.ds(PAD + nxl, XH), pl.ds(PAD + nxl, XH - 1)
+
+    def sideways(src, dst, side, number, device):
+        early = halo(facing, src, dst, number, device)
+        early.append(remote(PK.at[side], RK.at[1 - side], number + 2, device))
+        return early, halo(others, src, dst, number + 3, device)
+
+    leftward = sideways(first, from_right, 0, 0, {"gx": left})
+    rightward = sideways(last, from_left, 1, 5, {"gx": right})
+    partner = {"gz": 1 - gz}
+    planes = remote(S0.at[pl.ds(0, 5), facing, pl.ds(PAD, nxl)], S0.at[pl.ds(0, 5), across, pl.ds(PAD, nxl)], 10, partner)
+
+    def corner(at, number):
+        (uvw, pf) = at
+        return [remote(S0.at[motion, facing, uvw], S0.at[motion, across, uvw], number, partner),
+                remote(S0.at[state, facing, pf], S0.at[state, across, pf], number + 1, partner)]
+
+    corners = corner(from_left, 11), corner(from_right, 13)
+    weights = remote(FD, RD, 15, partner)
+    inner = remote(FM, RM, 16, partner)
+    strips = [remote(FE.at[side], RE.at[side], 17 + side, partner) for side in range(2)]
+    incoming = rightward, leftward
+    have = (has_left, has_right)
+
+    for n in range(5):
+        copies[n].wait()
+    G[2, mine] = M[...].astype(jnp.float32)
+    FX[mine] = G[1, mine] + G[0, mine]
+    end = PAD + nxl
+    PK[0, 0:4] = FX[PAD:PAD + 4]
+    PK[0, 4:7] = G[2, PAD:PAD + 3]
+    PK[0, 7:8] = G[0, PAD:PAD + 1]
+    PK[1, 0:4] = FX[end - 4:end]
+    PK[1, 4:7] = G[2, end - 3:end]
+    PK[1, 7:8] = G[0, end - 1:end]
+
+    @pl.when(gz == 0)
+    def _():
+        pl.semaphore_wait(barrier, 3)
+        pl.semaphore_signal(ready.at[0], inc=1, device_id=partner, device_id_type=MESH)
+
+    @pl.when(gz == 1)
+    def _():
+        pl.semaphore_wait(ready.at[0], 1)
+
+    def launch(group, flag):
+        @pl.when(flag)
+        def _():
+            for copy in group:
+                copy.start()
+
+    launch(leftward[0], odd == 1)
+    launch(rightward[0], odd == 0)
+    eager = lax.rem(gx + 1, 4) < 2
+    launch(leftward[1], (odd == 1) & eager)
+    launch(rightward[1], (odd == 0) & eager)
+    planes.start()
+
+
+    def dy(f):
+        axis = f.ndim - 1
+        lane = lax.broadcasted_iota(jnp.int32, f.shape, axis)
+        return (jnp.where(lane < ny - 1, pltpu.roll(f, ny - 1, axis), 0.0)
+                - jnp.where(lane > 0, pltpu.roll(f, 1, axis), 0.0))
+
+    def inside(start, height):
+        column = gx * nxl + lax.broadcasted_iota(jnp.int32, (height, ny), 0) + (start - PAD)
+        return (column >= 0) & (column < nx * nxl)
+
+    def plan(start, height):
+        c = slice(start, start + height)
+        A[0, c] = 0.5 * (FX[start + 1:start + height + 1] - FX[start - 1:start + height - 1])
+        A[1, c] = 0.5 * dy(FX[c])
+        A[2, c] = jnp.where(inside(start, height) & (G[2, c] > 0.0), 1.0, 0.0)
+        A[3, c] = jnp.where(G[2, c] == 1.0, FRICTION, 0.0)
+
+    def level_at(k, count):
+        return gz * nl + k - base + lax.broadcasted_iota(jnp.int32, (count, 1, ny), 0)
+
+    def stress(B, k, count, start, height):
+        at = pl.ds(k, count)
+        c = slice(start, start + height)
+        m, p = slice(start - 1, start + height - 1), slice(start + 1, start + height + 1)
+        above, below = pl.ds(k + 1, count), pl.ds(k - 1, count)
+        xx, vx, wx = (B[f, at, p] - B[f, at, m] for f in range(3))
+        uz, vz, zz = (B[f, above, c] - B[f, below, c] for f in range(3))
+        uy, yy, wy = (dy(B[f, at, c]) for f in range(3))
+        xy, xz, yz = uy + vx, uz + wx, vz + wy
+        twice = xx * xx + yy * yy + zz * zz
+        second = 0.0625 * (twice + twice + (xy * xy + xz * xz + yz * yz))
+        third = jnp.log2(S0[4, at, c] * (second + REGULAR)) * (1.0 / 3.0)
+        a = jnp.exp2(-third)
+        V[0, at, c] = (2.0 * STEP) * jnp.exp2(third)
+        V[1, at, c] = (0.25 * STEP) * a * (xx + yy + zz)
+        h = 0.25 * a
+        if height == 8:
+            h = jnp.where(jnp.broadcast_to(inside(start, height)[None], h.shape), h, 0.0)
+        g = 0.5 * h
+        T[0, at, c] = g * xz
+        T[1, at, c] = g * yz
+        T[2, at, c] = h * zz
+        T[3, at, c] = h * xx
+        T[4, at, c] = g * xy
+        T[5, at, c] = h * yy
+
+    def move(B, k, count, start, height):
+        at = pl.ds(k, count)
+        c = slice(start, start + height)
+        m, p = slice(start - 1, start + height - 1), slice(start + 1, start + height + 1)
+        above, below = pl.ds(k + 1, count), pl.ds(k - 1, count)
+        drag = jnp.where(level_at(k, count) == 0, 1.0, 0.0) * A[3, c][None]
+        u, v, press = B[0, at, c], B[1, at, c], B[3, at, c]
+        fx = ((T[3, at, p] - T[3, at, m]) + dy(T[4, at, c]) + (T[0, above, c] - T[0, below, c])
+              - 0.5 * (B[3, at, p] - B[3, at, m]) - A[0, c][None] - drag * u)
+        fy = ((T[4, at, p] - T[4, at, m]) + dy(T[5, at, c]) + (T[1, above, c] - T[1, below, c])
+              - 0.5 * dy(press) - A[1, c][None] - drag * v)
+        fz = ((T[0, at, p] - T[0, at, m]) + dy(T[1, at, c]) + (T[2, above, c] - T[2, below, c])
+              - 0.5 * (B[3, above, c] - B[3, below, c]))
+        step = V[0, at, c]
+        ice = jnp.broadcast_to(A[2, c][None], u.shape)
+        return [jnp.where(ice > 0.0, value, 0.0) for value in (
+            u + step * fx, v + step * fy, B[2, at, c] + step * fz, press - V[1, at, c])]
+
+    def blocks(start, count, most, step, area):
+        pieces = -(-count // most)
+        for n in range(pieces):
+            one, two = count * n // pieces, count * (n + 1) // pieces
+            step(start + one, two - one, *area)
+
+    def apart(reach, most, step, area):
+        blocks(1 + gz * (2 * ZH - reach), nl - ZH + reach, most, step, area)
+
+    def facing_part(reach, most, step, area):
+        low, high = 1 + nl - ZH + reach, 1 + ZH - reach
+        blocks(low + gz * (high - low), ZH, most, step, area)
+
+    def reached(reach, most, step, area):
+        low = 1 + nl - reach
+        blocks(low + gz * (1 + ZH - reach - low), 2 * (ZH - 4 + reach), most, step, area)
+
+    def rest(reach, most, step, area):
+        count = nl - reach
+        blocks(1 + gz * (ZH + nl - count), count, most, step, area)
+
+    def stress_first(*at):
+        stress(S0, *at)
+
+    def stress_last(*at):
+        stress(S1, *at)
+
+    def move_first(k, count, start, height):
+        for f, value in enumerate(move(S0, k, count, start, height)):
+            S1[f, pl.ds(k, count), start:start + height] = value
+
+    def move_last(k, count, start, height):
+        for f, value in enumerate(move(S1, k, count, start, height)):
+            flow_out[f, pl.ds(k - base, count), start:start + height] = value
+
+    middle = (PAD + 1, nxl - 2)
+    plan(*middle)
+    apart(3, 2, stress_first, middle)
+
+    copies[5].wait()
+    copies[6].wait()
+    total = jnp.zeros((nxl, ny), jnp.float32)
+    for k in reversed(range(nl)):
+        cell = DN[k]
+        DN[k] = total + 0.5 * cell
+        total = total + cell
+    FS[2, mine] = total
+
+    def dy(f):
+        axis = f.ndim - 1
+        lane = lax.broadcasted_iota(jnp.int32, f.shape, axis)
+        return (jnp.where(lane < ny - 1, pltpu.roll(f, ny - 1, axis), 0.0)
+                - jnp.where(lane > 0, pltpu.roll(f, 1, axis), 0.0))
+
+    def inside(start, height):
+        column = gx * nxl + lax.broadcasted_iota(jnp.int32, (height, ny), 0) + (start - PAD)
+        return (column >= 0) & (column < nx * nxl)
+
+    def plan(start, height):
+        c = slice(start, start + height)
+        A[0, c] = 0.5 * (FX[start + 1:start + height + 1] - FX[start - 1:start + height - 1])
+        A[1, c] = 0.5 * dy(FX[c])
+        A[2, c] = jnp.where(inside(start, height) & (M[c] > 0), 1.0, 0.0)
+        A[3, c] = jnp.where(M[c] == 1, FRICTION, 0.0)
+
+    def level_at(k, count):
+        return gz * nl + k - base + lax.broadcasted_iota(jnp.int32, (count, 1, ny), 0)
+
+    def stress(B, k, count, start, height):
+        at = pl.ds(k, count)
+        c = slice(start, start + height)
+        m, p = slice(start - 1, start + height - 1), slice(start + 1, start + height + 1)
+        above, below = pl.ds(k + 1, count), pl.ds(k - 1, count)
+        xx, vx, wx = (B[f, at, p] - B[f, at, m] for f in range(3))
+        uz, vz, zz = (B[f, above, c] - B[f, below, c] for f in range(3))
+        uy, yy, wy = (dy(B[f, at, c]) for f in range(3))
+        xy, xz, yz = uy + vx, uz + wx, vz + wy
+        twice = xx * xx + yy * yy + zz * zz
+        second = 0.0625 * (twice + twice + (xy * xy + xz * xz + yz * yz))
+        third = jnp.log2(S0[4, at, c] * (second + REGULAR)) * (1.0 / 3.0)
+        a = jnp.exp2(-third)
+        V[0, at, c] = (2.0 * STEP) * jnp.exp2(third)
+        V[1, at, c] = (0.25 * STEP) * a * (xx + yy + zz)
+        h = 0.25 * a
+        if height == 8:
+            h = jnp.where(jnp.broadcast_to(inside(start, height)[None], h.shape), h, 0.0)
+        if nz > 2:
+            level = level_at(k, count)
+            ok = jnp.where((level >= 0) & (level < levels_total), 1.0, 0.0)
+            h = jnp.where(jnp.broadcast_to(ok, h.shape) > 0.0, h, 0.0)
+        g = 0.5 * h
+        T[0, at, c] = g * xz
+        T[1, at, c] = g * yz
+        T[2, at, c] = h * zz
+        T[3, at, c] = h * xx
+        T[4, at, c] = g * xy
+        T[5, at, c] = h * yy
+
+    def move(B, k, count, start, height):
+        at = pl.ds(k, count)
+        c = slice(start, start + height)
+        m, p = slice(start - 1, start + height - 1), slice(start + 1, start + height + 1)
+        above, below = pl.ds(k + 1, count), pl.ds(k - 1, count)
+        level = level_at(k, count)
+        drag = jnp.where(level == 0, 1.0, 0.0) * A[3, c][None]
+        u, v, press = B[0, at, c], B[1, at, c], B[3, at, c]
+        fx = ((T[3, at, p] - T[3, at, m]) + dy(T[4, at, c]) + (T[0, above, c] - T[0, below, c])
+              - 0.5 * (B[3, at, p] - B[3, at, m]) - A[0, c][None] - drag * u)
+        fy = ((T[4, at, p] - T[4, at, m]) + dy(T[5, at, c]) + (T[1, above, c] - T[1, below, c])
+              - 0.5 * dy(press) - A[1, c][None] - drag * v)
+        fz = ((T[0, at, p] - T[0, at, m]) + dy(T[1, at, c]) + (T[2, above, c] - T[2, below, c])
+              - 0.5 * (B[3, above, c] - B[3, below, c]))
+        step = V[0, at, c]
+        ice = jnp.broadcast_to(A[2, c][None], u.shape)
+        if nz > 2:
+            ice = ice * jnp.where((level >= 0) & (level < levels_total), 1.0, 0.0)
+        return [jnp.where(ice > 0.0, value, 0.0) for value in (
+            u + step * fx, v + step * fy, B[2, at, c] + step * fz, press - V[1, at, c])]
+
+    def blocks(reach, most, step, areas):
+        start, count = span(reach)
+        pieces = -(-count // most)
+        for n in range(pieces):
+            one, two = count * n // pieces, count * (n + 1) // pieces
+            for area in areas:
+                step(start + one, two - one, *area)
+
+    def stress_first(*at):
+        stress(S0, *at)
+
+    def stress_last(*at):
+        stress(S1, *at)
+
+    def move_first(k, count, start, height):
+        for f, value in enumerate(move(S0, k, count, start, height)):
+            S1[f, pl.ds(k, count), start:start + height] = value
+
+    def move_last(k, count, start, height):
+        for f, value in enumerate(move(S1, k, count, start, height)):
+            flow_out[f, pl.ds(k - base, count), start:start + height] = value
+
+    middle = [(PAD + 1, nxl - 2)]
+    FX[mine] = G[1, mine] + G[0, mine]
+    plan(*middle[0])
+    for flag, group in ((has_down, upward), (has_up, downward)):
+        @pl.when(flag)
+        def _():
+            group[0].wait_recv()
+
+    blocks(3, 2, stress_first, middle)
+    blocks(2, 2, move_first, middle)
+    blocks(1, 2, stress_last, middle)
+
+    @pl.when(has_left)
+    def _():
+        for copy in rightward:
+            copy.wait_recv()
+
+    @pl.when(has_left & has_up)
+    def _():
+        upward[1].start()
+
+    @pl.when(has_left & has_down)
+    def _():
+        downward[1].start()
+
+    @pl.when(has_right)
+    def _():
+        for copy in leftward:
+            copy.wait_recv()
+
+    @pl.when(has_right & has_up)
+    def _():
+        upward[2].start()
+
+    @pl.when(has_right & has_down)
+    def _():
+        downward[2].start()
+
+    blocks(0, 2, move_last, middle)
+
+    ends = [(PAD - 4, 8), (PAD + nxl - 4, 8)]
+    for start in (PAD - 8, PAD + nxl):
+        strip = slice(start, start + 8)
+        FX[strip] = G[1, strip] + G[0, strip]
+    for area in ends:
+        plan(*area)
+    for flag, group in ((has_down, upward), (has_up, downward)):
+        @pl.when(flag & has_left)
+        def _():
+            group[1].wait_recv()
+
+        @pl.when(flag & has_right)
+        def _():
+            group[2].wait_recv()
+
+    blocks(3, 6, stress_first, ends)
+    blocks(2, 6, move_first, [(PAD - 5, 8), (PAD + nxl - 3, 8)])
+    blocks(1, 6, stress_last, ends)
+    blocks(0, 4, move_last, ends)
+    sum_u, sum_v = flow_out[0, 0, c], flow_out[1, 0, c]
+    for k in range(1, nl):
+        sum_u = sum_u + flow_out[0, k, c]
+        sum_v = sum_v + flow_out[1, k, c]
+    FS[0, c] = sum_u
+    FS[1, c] = sum_v
+
+    sums = [pltpu.make_async_remote_copy(
+        src_ref=FS.at[:, pl.ds(lo, width)], dst_ref=FR.at[off - 1, :, pl.ds(lo, width)],
+        send_sem=fsend.at[off - 1], recv_sem=frecv.at[off - 1],
+        device_id={"gz": lax.rem(gz + off, nz)}, device_id_type=MESH) for off in range(1, nz)]
+    for copy in sums:
+        copy.start()
+    above = jnp.zeros((nxl, ny), jnp.float32)
+    for off in range(1, nz):
+        sums[off - 1].wait_recv()
+        sum_u = sum_u + FR[off - 1, 0, c]
+        sum_v = sum_v + FR[off - 1, 1, c]
+        above = above + jnp.where(gz < off, 1.0, 0.0) * FR[off - 1, 2, mine]
+    part = G[0, c] * (1.0 / levels_total)
+    FX[c] = part * sum_u
+    flux_y = dy(part * sum_v)[8:8 + nxl]
+    spread = FX[PAD + 1:PAD + nxl + 1] - FX[PAD - 1:PAD + nxl - 1] + flux_y
+    fresh = G[0, mine] + TIME_STEP * (SM[...] - 0.5 * spread)
+    new_thickness[...] = fresh
+    weight = fresh * (1.0 / levels_total)
+    for k in range(nl):
+        overburden[k] = weight * (above + DN[k])
+
+    @pl.when(has_left)
+    def _():
+        for copy in leftward:
+            copy.wait_send()
+
+    @pl.when(has_right)
+    def _():
+        for copy in rightward:
+            copy.wait_send()
+
+    for flag, group in ((has_up, upward), (has_down, downward)):
+        @pl.when(flag)
+        def _():
+            group[0].wait_send()
+
+        @pl.when(flag & has_left)
+        def _():
+            group[1].wait_send()
+
+        @pl.when(flag & has_right)
+        def _():
+            group[2].wait_send()
+
+    for copy in sums:
+        copy.wait_send()
+
+
+def paired(nx, nl, nxl, flow, fluid, density, thickness, bed, smb, mask,
+           flow_out, new_thickness, overburden,
+           S0, S1, T, V, G, M, PK, RK, SM, DN, A, FX, FM, RM, FE, RE, FD, RD,
+           loc, ready, send, recv):
+    gx, gz = lax.axis_index("gx"), lax.axis_index("gz")
+    left, right = lax.rem(gx + nx - 1, nx), lax.rem(gx + 1, nx)
+    has_left, has_right = gx > 0, gx < nx - 1
+    odd = lax.rem(gx, 2)
+    near = gx + 1 - 2 * odd
+    far = lax.rem(gx + nx - 1 + 2 * odd, nx)
+    has_far = jnp.where(odd == 1, gx, nx - 1 - gx) < nx - 1
+    ny = flow.shape[-1]
+    levels_total = 2 * nl
+    depth, rows = S0.shape[1], S0.shape[2]
+    base = 1 + ZH * gz
+    own = pl.ds(base, nl)
+    facing = pl.ds(1 + nl - ZH + gz * (2 * ZH - nl), ZH)
+    others = pl.ds(1 + gz * 2 * ZH, nl - ZH)
+    across = pl.ds(1 + gz * nl, ZH)
+    mine = slice(PAD, PAD + nxl)
+
+    barrier = pltpu.get_barrier_semaphore()
+    pl.semaphore_signal(barrier, inc=1, device_id={"gx": near, "gz": 0}, device_id_type=MESH)
+
+    @pl.when(has_far)
+    def _():
+        pl.semaphore_signal(barrier, inc=1, device_id={"gx": far, "gz": 1}, device_id_type=MESH)
+
+    @pl.when(gz == 1)
+    def _():
+        pl.semaphore_signal(barrier, inc=1, device_id={"gz": 0}, device_id_type=MESH)
+
+    copies = [
+        pltpu.make_async_copy(flow, S0.at[pl.ds(0, 4), own, mine], loc.at[0]),
+        pltpu.make_async_copy(fluid, S0.at[4, own, mine], loc.at[1]),
+        pltpu.make_async_copy(thickness, G.at[0, mine], loc.at[2]),
+        pltpu.make_async_copy(bed, G.at[1, mine], loc.at[3]),
+        pltpu.make_async_copy(mask, M, loc.at[4]),
+        pltpu.make_async_copy(density, DN, loc.at[5]),
+        pltpu.make_async_copy(smb, SM, loc.at[6]),
+    ]
+    for copy in copies:
+        copy.start()
+
+    zrow = jnp.zeros((rows, ny), jnp.float32)
+    for k in (0, depth - 1):
+        for f in range(4):
+            S0[f, k] = zrow
+            S1[f, k] = zrow
+        for f in range(3):
+            T[f, k] = zrow
+
+    def outside_x(where):
+        strip = slice(PAD - 8, PAD) if where == 0 else slice(PAD + nxl, PAD + nxl + 8)
+        zero = jnp.zeros((8, ny), jnp.float32)
+
+        def one(k, _):
+            for f in range(4):
+                S0[f, k, strip] = zero
+            S0[4, k, strip] = zero + 1.0
+            return 0
+
+        lax.fori_loop(1, depth - 1, one, 0)
+        G[0, strip] = zero
+        G[2, strip] = zero
+        FX[strip] = zero
+
+    @pl.when(jnp.logical_not(has_left))
+    def _():
+        outside_x(0)
+
+    @pl.when(jnp.logical_not(has_right))
+    def _():
+        outside_x(1)
+
+    def remote(src, dst, number, device):
+        return pltpu.make_async_remote_copy(src_ref=src, dst_ref=dst, send_sem=send.at[number],
+                                            recv_sem=recv.at[number], device_id=device, device_id_type=MESH)
+
+    motion, state = pl.ds(0, 3), pl.ds(3, 2)
+
+    def halo(levels, src, dst, number, device):
+        (src_uvw, src_pf), (dst_uvw, dst_pf) = src, dst
+        return [remote(S0.at[motion, levels, src_uvw], S0.at[motion, levels, dst_uvw], number, device),
+                remote(S0.at[state, levels, src_pf], S0.at[state, levels, dst_pf], number + 1, device)]
+
+    first = pl.ds(PAD, XH), pl.ds(PAD, XH - 1)
+    last = pl.ds(PAD + nxl - XH, XH), pl.ds(PAD + nxl - XH + 1, XH - 1)
+    from_left = pl.ds(PAD - XH, XH), pl.ds(PAD - XH + 1, XH - 1)
+    from_right = pl.ds(PAD + nxl, XH), pl.ds(PAD + nxl, XH - 1)
+
+    def sideways(src, dst, side, number, device):
+        early = halo(facing, src, dst, number, device)
+        early.append(remote(PK.at[side], RK.at[1 - side], number + 2, device))
+        return early, halo(others, src, dst, number + 3, device)
+
+    leftward = sideways(first, from_right, 0, 0, {"gx": left})
+    rightward = sideways(last, from_left, 1, 5, {"gx": right})
+    partner = {"gz": 1 - gz}
+    planes = remote(S0.at[pl.ds(0, 5), facing, pl.ds(PAD, nxl)], S0.at[pl.ds(0, 5), across, pl.ds(PAD, nxl)], 10, partner)
+
+    def corner(at, number):
+        (uvw, pf) = at
+        return [remote(S0.at[motion, facing, uvw], S0.at[motion, across, uvw], number, partner),
+                remote(S0.at[state, facing, pf], S0.at[state, across, pf], number + 1, partner)]
+
+    corners = corner(from_left, 11), corner(from_right, 13)
+    weights = remote(FD, RD, 15, partner)
+    inner = remote(FM, RM, 16, partner)
+    strips = [remote(FE.at[side], RE.at[side], 17 + side, partner) for side in range(2)]
+    incoming = rightward, leftward
+    have = (has_left, has_right)
+
+    for n in range(5):
+        copies[n].wait()
+    G[2, mine] = M[...].astype(jnp.float32)
+    FX[mine] = G[1, mine] + G[0, mine]
+    end = PAD + nxl
+    PK[0, 0:4] = FX[PAD:PAD + 4]
+    PK[0, 4:7] = G[2, PAD:PAD + 3]
+    PK[0, 7:8] = G[0, PAD:PAD + 1]
+    PK[1, 0:4] = FX[end - 4:end]
+    PK[1, 4:7] = G[2, end - 3:end]
+    PK[1, 7:8] = G[0, end - 1:end]
+
+    @pl.when(gz == 0)
+    def _():
+        pl.semaphore_wait(barrier, 3)
+        pl.semaphore_signal(ready.at[0], inc=1, device_id=partner, device_id_type=MESH)
+
+    @pl.when(gz == 1)
+    def _():
+        pl.semaphore_wait(ready.at[0], 1)
+
+    def launch(group, flag):
+        @pl.when(flag)
+        def _():
+            for copy in group:
+                copy.start()
+
+    launch(leftward[0], odd == 1)
+    launch(rightward[0], odd == 0)
+    eager = lax.rem(gx + 1, 4) < 2
+    launch(leftward[1], (odd == 1) & eager)
+    launch(rightward[1], (odd == 0) & eager)
+    planes.start()
+
+    def dy(f):
+        axis = f.ndim - 1
+        lane = lax.broadcasted_iota(jnp.int32, f.shape, axis)
+        return (jnp.where(lane < ny - 1, pltpu.roll(f, ny - 1, axis), 0.0)
+                - jnp.where(lane > 0, pltpu.roll(f, 1, axis), 0.0))
+
+    def inside(start, height):
+        column = gx * nxl + lax.broadcasted_iota(jnp.int32, (height, ny), 0) + (start - PAD)
+        return (column >= 0) & (column < nx * nxl)
+
+    def plan(start, height):
+        c = slice(start, start + height)
+        A[0, c] = 0.5 * (FX[start + 1:start + height + 1] - FX[start - 1:start + height - 1])
+        A[1, c] = 0.5 * dy(FX[c])
+        A[2, c] = jnp.where(inside(start, height) & (G[2, c] > 0.0), 1.0, 0.0)
+        A[3, c] = jnp.where(G[2, c] == 1.0, FRICTION, 0.0)
+
+    def level_at(k, count):
+        return gz * nl + k - base + lax.broadcasted_iota(jnp.int32, (count, 1, ny), 0)
+
+    def stress(B, k, count, start, height):
+        at = pl.ds(k, count)
+        c = slice(start, start + height)
+        m, p = slice(start - 1, start + height - 1), slice(start + 1, start + height + 1)
+        above, below = pl.ds(k + 1, count), pl.ds(k - 1, count)
+        xx, vx, wx = (B[f, at, p] - B[f, at, m] for f in range(3))
+        uz, vz, zz = (B[f, above, c] - B[f, below, c] for f in range(3))
+        uy, yy, wy = (dy(B[f, at, c]) for f in range(3))
+        xy, xz, yz = uy + vx, uz + wx, vz + wy
+        twice = xx * xx + yy * yy + zz * zz
+        second = 0.0625 * (twice + twice + (xy * xy + xz * xz + yz * yz))
+        third = jnp.log2(S0[4, at, c] * (second + REGULAR)) * (1.0 / 3.0)
+        a = jnp.exp2(-third)
+        V[0, at, c] = (2.0 * STEP) * jnp.exp2(third)
+        V[1, at, c] = (0.25 * STEP) * a * (xx + yy + zz)
+        h = 0.25 * a
+        if height == 8:
+            h = jnp.where(jnp.broadcast_to(inside(start, height)[None], h.shape), h, 0.0)
+        g = 0.5 * h
+        T[0, at, c] = g * xz
+        T[1, at, c] = g * yz
+        T[2, at, c] = h * zz
+        T[3, at, c] = h * xx
+        T[4, at, c] = g * xy
+        T[5, at, c] = h * yy
+
+    def move(B, k, count, start, height):
+        at = pl.ds(k, count)
+        c = slice(start, start + height)
+        m, p = slice(start - 1, start + height - 1), slice(start + 1, start + height + 1)
+        above, below = pl.ds(k + 1, count), pl.ds(k - 1, count)
+        drag = jnp.where(level_at(k, count) == 0, 1.0, 0.0) * A[3, c][None]
+        u, v, press = B[0, at, c], B[1, at, c], B[3, at, c]
+        fx = ((T[3, at, p] - T[3, at, m]) + dy(T[4, at, c]) + (T[0, above, c] - T[0, below, c])
+              - 0.5 * (B[3, at, p] - B[3, at, m]) - A[0, c][None] - drag * u)
+        fy = ((T[4, at, p] - T[4, at, m]) + dy(T[5, at, c]) + (T[1, above, c] - T[1, below, c])
+              - 0.5 * dy(press) - A[1, c][None] - drag * v)
+        fz = ((T[0, at, p] - T[0, at, m]) + dy(T[1, at, c]) + (T[2, above, c] - T[2, below, c])
+              - 0.5 * (B[3, above, c] - B[3, below, c]))
+        step = V[0, at, c]
+        ice = jnp.broadcast_to(A[2, c][None], u.shape)
+        return [jnp.where(ice > 0.0, value, 0.0) for value in (
+            u + step * fx, v + step * fy, B[2, at, c] + step * fz, press - V[1, at, c])]
+
+    def blocks(start, count, most, step, area):
+        pieces = -(-count // most)
+        for n in range(pieces):
+            one, two = count * n // pieces, count * (n + 1) // pieces
+            step(start + one, two - one, *area)
+
+    def apart(reach, most, step, area):
+        blocks(1 + gz * (2 * ZH - reach), nl - ZH + reach, most, step, area)
+
+    def facing_part(reach, most, step, area):
+        low, high = 1 + nl - ZH + reach, 1 + ZH - reach
+        blocks(low + gz * (high - low), ZH, most, step, area)
+
+    def reached(reach, most, step, area):
+        low = 1 + nl - reach
+        blocks(low + gz * (1 + ZH - reach - low), 2 * (ZH - 4 + reach), most, step, area)
+
+    def rest(reach, most, step, area):
+        count = nl - reach
+        blocks(1 + gz * (ZH + nl - count), count, most, step, area)
+
+    def stress_first(*at):
+        stress(S0, *at)
+
+    def stress_last(*at):
+        stress(S1, *at)
+
+    def move_first(k, count, start, height):
+        for f, value in enumerate(move(S0, k, count, start, height)):
+            S1[f, pl.ds(k, count), start:start + height] = value
+
+    def move_last(k, count, start, height):
+        for f, value in enumerate(move(S1, k, count, start, height)):
+            flow_out[f, pl.ds(k - base, count), start:start + height] = value
+
+    middle = (PAD + 1, nxl - 2)
+    plan(*middle)
+    apart(3, 2, stress_first, middle)
+
+    @pl.when(has_far & (gz == 1))
+    def _():
+        pl.semaphore_wait(barrier, 2)
+        pl.semaphore_signal(ready.at[1], inc=1, device_id=partner, device_id_type=MESH)
+
+    @pl.when(has_far & (gz == 0))
+    def _():
+        pl.semaphore_wait(ready.at[1], 1)
+
+    launch(rightward[0], (odd == 1) & has_right)
+    launch(leftward[0], (odd == 0) & has_left)
+    launch(leftward[1], (odd == 1) & jnp.logical_not(eager))
+    launch(rightward[1], (odd == 0) & jnp.logical_not(eager))
+    launch(rightward[1], (odd == 1) & has_right)
+    launch(leftward[1], (odd == 0) & has_left)
+
+    copies[5].wait()
+    copies[6].wait()
+    total = jnp.zeros((nxl, ny), jnp.float32)
+    for k in reversed(range(nl)):
+        cell = DN[k]
+        DN[k] = total + 0.5 * cell
+        total = total + cell
+    FD[...] = total
+    weights.start()
+
+    apart(2, 2, move_first, middle)
+    apart(1, 2, stress_last, middle)
+    apart(0, 2, move_last, middle)
+    planes.wait_recv()
+    facing_part(3, 2, stress_first, middle)
+
+    def forward(side):
+        @pl.when(have[side])
+        def _():
+            for copy in incoming[side][0][:2]:
+                copy.wait_recv()
+            for copy in corners[side]:
+                copy.start()
+
+    crossed = (lax.rem(gx, 4) == 2) & (gx > 2)
+    left_leads = (gx == 0) | (((odd == 1) | crossed) & has_right)
+
+    def by_arrival(step):
+        @pl.when(left_leads)
+        def _():
+            step(0, 1)
+
+        @pl.when(jnp.logical_not(left_leads))
+        def _():
+            step(1, 0)
+
+    facing_part(2, 2, move_first, middle)
+    facing_part(1, 2, stress_last, middle)
+    facing_part(0, 2, move_last, middle)
+
+    by_arrival(lambda lead, other: forward(lead))
+
+    def depth_sum(f, c):
+        value = flow_out[f, 0, c]
+        for k in range(1, nl):
+            value = value + flow_out[f, k, c]
+        return value
+
+    for f in range(2):
+        FM[f] = depth_sum(f, mine)
+    inner.start()
+
+    edges = [((PAD - 4, 8), (PAD - 5, 8)), ((PAD + nxl - 4, 8), (PAD + nxl - 3, 8))]
+
+    def approach(side):
+        area, shifted = edges[side]
+
+        @pl.when(have[side])
+        def _():
+            incoming[side][0][2].wait_recv()
+            at = PAD if side == 0 else end
+            for row in range(4):
+                to = at - 4 + row if side == 0 else at + row
+                FX[to:to + 1] = RK[side, row:row + 1]
+            for row in range(3):
+                to = at - 3 + row if side == 0 else at + row
+                G[2, to:to + 1] = RK[side, 4 + row:5 + row]
+            to = at - 1 if side == 0 else at
+            G[0, to:to + 1] = RK[side, 7:8]
+            for copy in corners[side]:
+                copy.wait_recv()
+
+        plan(*area)
+        reached(3, 3, stress_first, area)
+        reached(2, 4, move_first, shifted)
+        reached(1, 4, stress_last, area)
+
+    def finish(side):
+        area, shifted = edges[side]
+
+        @pl.when(have[side])
+        def _():
+            for copy in incoming[side][1]:
+                copy.wait_recv()
+
+        rest(3, 5, stress_first, area)
+        rest(2, 6, move_first, shifted)
+        rest(1, 4, stress_last, area)
+        rest(0, 4, move_last, area)
+        wide = slice(PAD - 8, PAD + 8) if side == 0 else slice(PAD + nxl - 8, PAD + nxl + 8)
+        for f in range(2):
+            FE[side, f] = depth_sum(f, wide)
+        strips[side].start()
+
+    def both(lead, other):
+        forward(other)
+        approach(lead)
+        finish(lead)
+        approach(other)
+        finish(other)
+
+    by_arrival(both)
+
+    def settle(start, height, sum_v):
+        c = slice(start, start + height)
+        o = slice(start - PAD, start - PAD + height)
+        flux_y = dy(G[0, c] * (1.0 / levels_total) * sum_v)
+        spread = FX[start + 1:start + height + 1] - FX[start - 1:start + height - 1] + flux_y
+        fresh = G[0, c] + TIME_STEP * (SM[o] - 0.5 * spread)
+        new_thickness[o] = fresh
+        weight = fresh * (1.0 / levels_total)
+        above = jnp.where(gz == 0, 1.0, 0.0) * RD[o]
+        for k in range(nl):
+            overburden[k, o] = weight * (above + DN[k, o])
+
+    weights.wait_recv()
+    inner.wait_recv()
+    FX[mine] = G[0, mine] * (1.0 / levels_total) * (FM[0] + RM[0])
+    settle(PAD + 8, nxl - 16, FM[1, 8:nxl - 8] + RM[1, 8:nxl - 8])
+    for side in range(2):
+        strips[side].wait_recv()
+        begin = PAD - 8 if side == 0 else PAD + nxl - 8
+        wide = slice(begin, begin + 16)
+        FX[wide] = G[0, wide] * (1.0 / levels_total) * (FE[side, 0] + RE[side, 0])
+        inward = slice(8, 16) if side == 0 else slice(0, 8)
+        settle(PAD if side == 0 else PAD + nxl - 8, 8, FE[side, 1, inward] + RE[side, 1, inward])
+
+    for side, group in ((0, leftward), (1, rightward)):
+        @pl.when(have[side])
+        def _():
+            for copy in (*group[0], *group[1], *corners[side]):
+                copy.wait_send()
+
+    for copy in (planes, weights, inner, *strips):
+        copy.wait_send()
+
+
 def write(nxl, held, fresh, weight, flow_out, new_thickness, overburden, done):
     copies = [
         pltpu.make_async_copy(held.at[:, :, pl.ds(PAD, nxl)], flow_out, done.at[0]),
@@ -404,20 +1275,32 @@
         rows = nxl + 2 * PAD
         f32 = jnp.float32
         vmem = pl.BlockSpec(memory_space=pltpu.VMEM)
-        held, fresh, weight = pl.pallas_call(
-            functools.partial(kernel, nx, nz, nl, nxl),
-            out_shape=(
-                pltpu.VMEM((4, nl, rows, ny), f32),
-                pltpu.VMEM(thickness.shape, f32),
-                pltpu.VMEM(density.shape, f32),
-            ),
-            in_specs=[pl.BlockSpec(memory_space=pl.ANY)] * 7,
-            out_specs=(vmem, vmem, vmem),
-            scratch_shapes=[
-                pltpu.VMEM((5, depth, rows, ny), f32),
-                pltpu.VMEM((4, depth, rows, ny), f32),
-                pltpu.VMEM((6, depth, rows, ny), f32),
-                pltpu.VMEM((2, depth, rows, ny), f32),
+        block = [pltpu.VMEM((n, depth, rows, ny), f32) for n in (5, 4, 6, 2)]
+        if nz == 2 and nx % 2 == 0 and nl > ZH and nxl >= 24:
+            body_of = functools.partial(paired, nx, nl, nxl)
+            scratch = block + [
+                pltpu.VMEM((3, rows, ny), f32),
+                pltpu.VMEM((nxl, ny), jnp.int32),
+                pltpu.VMEM((2, 8, ny), f32),
+                pltpu.VMEM((2, 8, ny), f32),
+                pltpu.VMEM((nxl, ny), f32),
+                pltpu.VMEM((nl, nxl, ny), f32),
+                pltpu.VMEM((4, rows, ny), f32),
+                pltpu.VMEM((rows, ny), f32),
+                pltpu.VMEM((2, nxl, ny), f32),
+                pltpu.VMEM((2, nxl, ny), f32),
+                pltpu.VMEM((2, 2, 16, ny), f32),
+                pltpu.VMEM((2, 2, 16, ny), f32),
+                pltpu.VMEM((nxl, ny), f32),
+                pltpu.VMEM((nxl, ny), f32),
+                pltpu.SemaphoreType.DMA((7,)),
+                pltpu.SemaphoreType.REGULAR((2,)),
+                pltpu.SemaphoreType.DMA((19,)),
+                pltpu.SemaphoreType.DMA((19,)),
+            ]
+        else:
+            body_of = functools.partial(kernel, nx, nz, nl, nxl)
+            scratch = block + [
                 pltpu.VMEM((2, rows, ny), f32),
                 pltpu.VMEM((rows, ny), jnp.int32),
                 pltpu.VMEM((nxl, ny), f32),
@@ -431,7 +1314,17 @@
                 pltpu.SemaphoreType.DMA((12,)),
                 pltpu.SemaphoreType.DMA((nz - 1,)),
                 pltpu.SemaphoreType.DMA((nz - 1,)),
-            ],
+            ]
+        held, fresh, weight = pl.pallas_call(
+            body_of,
+            out_shape=(
+                pltpu.VMEM((4, nl, rows, ny), f32),
+                pltpu.VMEM(thickness.shape, f32),
+                pltpu.VMEM(density.shape, f32),
+            ),
+            in_specs=[pl.BlockSpec(memory_space=pl.ANY)] * 7,
+            out_specs=(vmem, vmem, vmem),
+            scratch_shapes=scratch,
             compiler_params=pltpu.CompilerParams(collective_id=0, has_side_effects=True),
         )(flow, fluid, density, thickness, bed, smb, mask)
         anywhere = pl.BlockSpec(memory_space=pl.ANY)

time: 13.6 us -> 13.2 us (0.971)
  Pallas kernels: 12.8 us -> 12.4 us
    pallas_call x1, Pallas kernels: 11.9 us -> 11.5 us  [body(): pl.pallas_call(body_of, out_shape=(pltpu.VMEM((4, nl, rows, ny), f32), pl...]
where the time goes in v1:
time: 13.2 us; the launch traced here: 13 us
  Pallas kernels  12.4 us (94%)
  between operations  0.64 us (5%)
    pallas_call x1, Pallas kernels, body(): pl.pallas_call(body_of, out_shape=(pltpu.VMEM((4, nl, rows, ny), f32), pl...  11.5 us
    pallas_call x1, Pallas kernels, body(): pl.pallas_call(functools.partial(write, nxl), out_shape=(jax.ShapeDtypeSt...  0.86 us

profile of v1, /device:TPU:29, one launch (start us, length us, event | category | flops | bytes accessed | tf_op | source)
XLA Modules:
  0.0 13.0 jit_solution(7157900176464809658)
XLA Ops:
  0.6 11.5 %shard_map.94 = (f32[4,8,64,128]{3,2,1,0:T(8,128)S(1)}, f32[32,128]{1,0:T(8,128)S(1)}, f32[8,32,128]{2,1,0:T(8,128)S(1)}) custom-call(f32[4,8,32,128]{3,2,1,0:T(8,128)} %flow.1, f32[8,32,128]{2,1,0:T(8,128)} %fluid.1, f32[8,32,128]{2,1,0:T(8,128)} %density.1, f32[32,128]{1,0:T(8,128)} %thickness.1, f32[32,128]{1,0:T(8,128)} %bed.1, f32[32,128]{1,0:T(8,128)} %smb.1, ...), custom_call_target="tpu_custom_call" | custom-call | tf_op jit(solution)/shard_map/pallas_call | solution.py:1318
  12.2 0.9 %shard_map.95 = (f32[4,8,32,128]{3,2,1,0:T(8,128)}, f32[32,128]{1,0:T(8,128)}, f32[8,32,128]{2,1,0:T(8,128)}) custom-call(f32[4,8,64,128]{3,2,1,0:T(8,128)S(1)} %get-tuple-element.6.held, f32[32,128]{1,0:T(8,128)S(1)} %get-tuple-element.7.fresh, f32[8,32,128]{2,1,0:T(8,128)S(1)} %get-tuple-element.8.weight), custom_call_target="tpu_custom_call" | custom-call | tf_op jit(solution)/shard_map/pallas_call | solution.py:1331

commit v2 on v0

--- a/solution.py
+++ b/solution.py
@@ -383,6 +383,392 @@
         copy.wait_send()
 
 
+def paired(nx, nl, nxl, flow, fluid, density, thickness, bed, smb, mask,
+           flow_out, new_thickness, overburden,
+           S0, S1, T, V, G, M, PK, RK, SM, DN, A, FX, FM, RM, FE, RE, FD, RD,
+           loc, send, recv):
+    gx, gz = lax.axis_index("gx"), lax.axis_index("gz")
+    left, right = lax.rem(gx + nx - 1, nx), lax.rem(gx + 1, nx)
+    has_left, has_right = gx > 0, gx < nx - 1
+    odd = lax.rem(gx, 2)
+    near = gx + 1 - 2 * odd
+    far = lax.rem(gx + nx - 1 + 2 * odd, nx)
+    has_far = jnp.where(odd == 1, gx, nx - 1 - gx) < nx - 1
+    ny = flow.shape[-1]
+    levels_total = 2 * nl
+    depth, rows = S0.shape[1], S0.shape[2]
+    base = 1 + ZH * gz
+    own = pl.ds(base, nl)
+    facing = pl.ds(1 + nl - ZH + gz * (2 * ZH - nl), ZH)
+    others = pl.ds(1 + gz * 2 * ZH, nl - ZH)
+    across = pl.ds(1 + gz * nl, ZH)
+    mine = slice(PAD, PAD + nxl)
+
+    barrier = pltpu.get_barrier_semaphore()
+    pl.semaphore_signal(barrier, inc=1, device_id={"gx": near}, device_id_type=MESH)
+    pl.semaphore_signal(barrier, inc=1, device_id={"gz": 1 - gz}, device_id_type=MESH)
+
+    @pl.when(has_far)
+    def _():
+        pl.semaphore_signal(barrier, inc=1, device_id={"gx": far}, device_id_type=MESH)
+
+    copies = [
+        pltpu.make_async_copy(flow, S0.at[pl.ds(0, 4), own, mine], loc.at[0]),
+        pltpu.make_async_copy(fluid, S0.at[4, own, mine], loc.at[1]),
+        pltpu.make_async_copy(thickness, G.at[0, mine], loc.at[2]),
+        pltpu.make_async_copy(bed, G.at[1, mine], loc.at[3]),
+        pltpu.make_async_copy(mask, M, loc.at[4]),
+        pltpu.make_async_copy(density, DN, loc.at[5]),
+        pltpu.make_async_copy(smb, SM, loc.at[6]),
+    ]
+    for copy in copies:
+        copy.start()
+
+    zrow = jnp.zeros((rows, ny), jnp.float32)
+    for k in (0, depth - 1):
+        for f in range(4):
+            S0[f, k] = zrow
+            S1[f, k] = zrow
+        for f in range(3):
+            T[f, k] = zrow
+
+    def outside_x(where):
+        strip = slice(PAD - 8, PAD) if where == 0 else slice(PAD + nxl, PAD + nxl + 8)
+        zero = jnp.zeros((8, ny), jnp.float32)
+
+        def one(k, _):
+            for f in range(4):
+                S0[f, k, strip] = zero
+            S0[4, k, strip] = zero + 1.0
+            return 0
+
+        lax.fori_loop(1, depth - 1, one, 0)
+        G[0, strip] = zero
+        G[2, strip] = zero
+        FX[strip] = zero
+
+    @pl.when(jnp.logical_not(has_left))
+    def _():
+        outside_x(0)
+
+    @pl.when(jnp.logical_not(has_right))
+    def _():
+        outside_x(1)
+
+    def remote(src, dst, number, device):
+        return pltpu.make_async_remote_copy(src_ref=src, dst_ref=dst, send_sem=send.at[number],
+                                            recv_sem=recv.at[number], device_id=device, device_id_type=MESH)
+
+    motion, state = pl.ds(0, 3), pl.ds(3, 2)
+
+    def halo(levels, src, dst, number, device):
+        (src_uvw, src_pf), (dst_uvw, dst_pf) = src, dst
+        return [remote(S0.at[motion, levels, src_uvw], S0.at[motion, levels, dst_uvw], number, device),
+                remote(S0.at[state, levels, src_pf], S0.at[state, levels, dst_pf], number + 1, device)]
+
+    first = pl.ds(PAD, XH), pl.ds(PAD, XH - 1)
+    last = pl.ds(PAD + nxl - XH, XH), pl.ds(PAD + nxl - XH + 1, XH - 1)
+    from_left = pl.ds(PAD - XH, XH), pl.ds(PAD - XH + 1, XH - 1)
+    from_right = pl.ds(PAD + nxl, XH), pl.ds(PAD + nxl, XH - 1)
+
+    def sideways(src, dst, side, number, device):
+        early = halo(facing, src, dst, number, device)
+        early.append(remote(PK.at[side], RK.at[1 - side], number + 2, device))
+        return early, halo(others, src, dst, number + 3, device)
+
+    leftward = sideways(first, from_right, 0, 0, {"gx": left})
+    rightward = sideways(last, from_left, 1, 5, {"gx": right})
+    partner = {"gz": 1 - gz}
+    planes = remote(S0.at[pl.ds(0, 5), facing, pl.ds(PAD, nxl)], S0.at[pl.ds(0, 5), across, pl.ds(PAD, nxl)], 10, partner)
+
+    def corner(at, number):
+        (uvw, pf) = at
+        return [remote(S0.at[motion, facing, uvw], S0.at[motion, across, uvw], number, partner),
+                remote(S0.at[state, facing, pf], S0.at[state, across, pf], number + 1, partner)]
+
+    corners = corner(from_left, 11), corner(from_right, 13)
+    weights = remote(FD, RD, 15, partner)
+    inner = remote(FM, RM, 16, partner)
+    strips = [remote(FE.at[side], RE.at[side], 17 + side, partner) for side in range(2)]
+    incoming = rightward, leftward
+    have = (has_left, has_right)
+
+    for n in range(5):
+        copies[n].wait()
+    G[2, mine] = M[...].astype(jnp.float32)
+    FX[mine] = G[1, mine] + G[0, mine]
+    end = PAD + nxl
+    PK[0, 0:4] = FX[PAD:PAD + 4]
+    PK[0, 4:7] = G[2, PAD:PAD + 3]
+    PK[0, 7:8] = G[0, PAD:PAD + 1]
+    PK[1, 0:4] = FX[end - 4:end]
+    PK[1, 4:7] = G[2, end - 3:end]
+    PK[1, 7:8] = G[0, end - 1:end]
+
+    pl.semaphore_wait(barrier, 2 + jnp.where(has_far, 1, 0))
+
+    def launch(group, flag):
+        @pl.when(flag)
+        def _():
+            for copy in group:
+                copy.start()
+
+    launch(leftward[0], odd == 1)
+    launch(rightward[0], odd == 0)
+    eager = lax.rem(gx + 1, 4) < 2
+    launch(leftward[1], (odd == 1) & eager)
+    launch(rightward[1], (odd == 0) & eager)
+    planes.start()
+
+    launch(rightward[0], (odd == 1) & has_right)
+    launch(leftward[0], (odd == 0) & has_left)
+    launch(leftward[1], (odd == 1) & jnp.logical_not(eager))
+    launch(rightward[1], (odd == 0) & jnp.logical_not(eager))
+    launch(rightward[1], (odd == 1) & has_right)
+    launch(leftward[1], (odd == 0) & has_left)
+
+
+    def dy(f):
+        axis = f.ndim - 1
+        lane = lax.broadcasted_iota(jnp.int32, f.shape, axis)
+        return (jnp.where(lane < ny - 1, pltpu.roll(f, ny - 1, axis), 0.0)
+                - jnp.where(lane > 0, pltpu.roll(f, 1, axis), 0.0))
+
+    def inside(start, height):
+        column = gx * nxl + lax.broadcasted_iota(jnp.int32, (height, ny), 0) + (start - PAD)
+        return (column >= 0) & (column < nx * nxl)
+
+    def plan(start, height):
+        c = slice(start, start + height)
+        A[0, c] = 0.5 * (FX[start + 1:start + height + 1] - FX[start - 1:start + height - 1])
+        A[1, c] = 0.5 * dy(FX[c])
+        A[2, c] = jnp.where(inside(start, height) & (G[2, c] > 0.0), 1.0, 0.0)
+        A[3, c] = jnp.where(G[2, c] == 1.0, FRICTION, 0.0)
+
+    def level_at(k, count):
+        return gz * nl + k - base + lax.broadcasted_iota(jnp.int32, (count, 1, ny), 0)
+
+    def stress(B, k, count, start, height):
+        at = pl.ds(k, count)
+        c = slice(start, start + height)
+        m, p = slice(start - 1, start + height - 1), slice(start + 1, start + height + 1)
+        above, below = pl.ds(k + 1, count), pl.ds(k - 1, count)
+        xx, vx, wx = (B[f, at, p] - B[f, at, m] for f in range(3))
+        uz, vz, zz = (B[f, above, c] - B[f, below, c] for f in range(3))
+        uy, yy, wy = (dy(B[f, at, c]) for f in range(3))
+        xy, xz, yz = uy + vx, uz + wx, vz + wy
+        twice = xx * xx + yy * yy + zz * zz
+        second = 0.0625 * (twice + twice + (xy * xy + xz * xz + yz * yz))
+        third = jnp.log2(S0[4, at, c] * (second + REGULAR)) * (1.0 / 3.0)
+        a = jnp.exp2(-third)
+        V[0, at, c] = (2.0 * STEP) * jnp.exp2(third)
+        V[1, at, c] = (0.25 * STEP) * a * (xx + yy + zz)
+        h = 0.25 * a
+        if height == 8:
+            h = jnp.where(jnp.broadcast_to(inside(start, height)[None], h.shape), h, 0.0)
+        g = 0.5 * h
+        q = 0.5 * B[3, at, c]
+        T[0, at, c] = g * xz
+        T[1, at, c] = g * yz
+        T[2, at, c] = h * zz - q
+        T[3, at, c] = h * xx - q
+        T[4, at, c] = g * xy
+        T[5, at, c] = h * yy - q
+
+    def move(B, k, count, start, height):
+        at = pl.ds(k, count)
+        c = slice(start, start + height)
+        m, p = slice(start - 1, start + height - 1), slice(start + 1, start + height + 1)
+        above, below = pl.ds(k + 1, count), pl.ds(k - 1, count)
+        drag = jnp.where(level_at(k, count) == 0, 1.0, 0.0) * A[3, c][None]
+        u, v, press = B[0, at, c], B[1, at, c], B[3, at, c]
+        fx = ((T[3, at, p] - T[3, at, m]) + dy(T[4, at, c]) + (T[0, above, c] - T[0, below, c])
+              - A[0, c][None] - drag * u)
+        fy = ((T[4, at, p] - T[4, at, m]) + dy(T[5, at, c]) + (T[1, above, c] - T[1, below, c])
+              - A[1, c][None] - drag * v)
+        fz = ((T[0, at, p] - T[0, at, m]) + dy(T[1, at, c]) + (T[2, above, c] - T[2, below, c]))
+        step = V[0, at, c]
+        ice = jnp.broadcast_to(A[2, c][None], u.shape)
+        return [jnp.where(ice > 0.0, value, 0.0) for value in (
+            u + step * fx, v + step * fy, B[2, at, c] + step * fz, press - V[1, at, c])]
+
+    def blocks(start, count, most, step, area):
+        pieces = -(-count // most)
+        for n in range(pieces):
+            one, two = count * n // pieces, count * (n + 1) // pieces
+            step(start + one, two - one, *area)
+
+    def apart(reach, most, step, area):
+        blocks(1 + gz * (2 * ZH - reach), nl - ZH + reach, most, step, area)
+
+    def facing_part(reach, most, step, area):
+        low, high = 1 + nl - ZH + reach, 1 + ZH - reach
+        blocks(low + gz * (high - low), ZH, most, step, area)
+
+    def reached(reach, most, step, area):
+        low = 1 + nl - reach
+        blocks(low + gz * (1 + ZH - reach - low), 2 * (ZH - 4 + reach), most, step, area)
+
+    def rest(reach, most, step, area):
+        count = nl - reach
+        blocks(1 + gz * (ZH + nl - count), count, most, step, area)
+
+    def stress_first(*at):
+        stress(S0, *at)
+
+    def stress_last(*at):
+        stress(S1, *at)
+
+    def move_first(k, count, start, height):
+        for f, value in enumerate(move(S0, k, count, start, height)):
+            S1[f, pl.ds(k, count), start:start + height] = value
+
+    def move_last(k, count, start, height):
+        for f, value in enumerate(move(S1, k, count, start, height)):
+            flow_out[f, pl.ds(k - base, count), start:start + height] = value
+
+    middle = (PAD + 1, nxl - 2)
+    plan(*middle)
+    apart(3, 2, stress_first, middle)
+
+    copies[5].wait()
+    copies[6].wait()
+    total = jnp.zeros((nxl, ny), jnp.float32)
+    for k in reversed(range(nl)):
+        cell = DN[k]
+        DN[k] = total + 0.5 * cell
+        total = total + cell
+    FD[...] = total
+    weights.start()
+
+    apart(2, 2, move_first, middle)
+    apart(1, 2, stress_last, middle)
+    apart(0, 2, move_last, middle)
+    planes.wait_recv()
+    facing_part(3, 2, stress_first, middle)
+
+    def forward(side):
+        @pl.when(have[side])
+        def _():
+            for copy in incoming[side][0][:2]:
+                copy.wait_recv()
+            for copy in corners[side]:
+                copy.start()
+
+    place = lax.rem(gx, 4)
+    crossed = ((place == 2) & (gx > 2)) | ((place == 1) & (gx > 1) & (gx < nx - 3))
+    left_leads = (gx == 0) | (((odd == 1) != crossed) & has_right)
+
+    def by_arrival(step):
+        @pl.when(left_leads)
+        def _():
+            step(0, 1)
+
+        @pl.when(jnp.logical_not(left_leads))
+        def _():
+            step(1, 0)
+
+    facing_part(2, 2, move_first, middle)
+    facing_part(1, 2, stress_last, middle)
+    facing_part(0, 2, move_last, middle)
+
+    by_arrival(lambda lead, other: forward(lead))
+
+    def depth_sum(f, c):
+        value = flow_out[f, 0, c]
+        for k in range(1, nl):
+            value = value + flow_out[f, k, c]
+        return value
+
+    for f in range(2):
+        FM[f] = depth_sum(f, mine)
+    inner.start()
+
+    edges = [((PAD - 4, 8), (PAD - 5, 8)), ((PAD + nxl - 4, 8), (PAD + nxl - 3, 8))]
+
+    def approach(side):
+        area, shifted = edges[side]
+
+        @pl.when(have[side])
+        def _():
+            incoming[side][0][2].wait_recv()
+            at = PAD if side == 0 else end
+            for row in range(4):
+                to = at - 4 + row if side == 0 else at + row
+                FX[to:to + 1] = RK[side, row:row + 1]
+            for row in range(3):
+                to = at - 3 + row if side == 0 else at + row
+                G[2, to:to + 1] = RK[side, 4 + row:5 + row]
+            to = at - 1 if side == 0 else at
+            G[0, to:to + 1] = RK[side, 7:8]
+            for copy in corners[side]:
+                copy.wait_recv()
+
+        plan(*area)
+        reached(3, 3, stress_first, area)
+        reached(2, 4, move_first, shifted)
+        reached(1, 4, stress_last, area)
+
+    def finish(side):
+        area, shifted = edges[side]
+
+        @pl.when(have[side])
+        def _():
+            for copy in incoming[side][1]:
+                copy.wait_recv()
+
+        rest(3, 5, stress_first, area)
+        rest(2, 6, move_first, shifted)
+        rest(1, 4, stress_last, area)
+        rest(0, 4, move_last, area)
+        wide = slice(PAD - 8, PAD + 8) if side == 0 else slice(PAD + nxl - 8, PAD + nxl + 8)
+        for f in range(2):
+            FE[side, f] = depth_sum(f, wide)
+        strips[side].start()
+
+    def both(lead, other):
+        forward(other)
+        approach(lead)
+        finish(lead)
+        approach(other)
+        finish(other)
+
+    by_arrival(both)
+
+    def settle(start, height, sum_v):
+        c = slice(start, start + height)
+        o = slice(start - PAD, start - PAD + height)
+        flux_y = dy(G[0, c] * (1.0 / levels_total) * sum_v)
+        spread = FX[start + 1:start + height + 1] - FX[start - 1:start + height - 1] + flux_y
+        fresh = G[0, c] + TIME_STEP * (SM[o] - 0.5 * spread)
+        new_thickness[o] = fresh
+        weight = fresh * (1.0 / levels_total)
+        above = jnp.where(gz == 0, 1.0, 0.0) * RD[o]
+        for k in range(nl):
+            overburden[k, o] = weight * (above + DN[k, o])
+
+    weights.wait_recv()
+    inner.wait_recv()
+    FX[mine] = G[0, mine] * (1.0 / levels_total) * (FM[0] + RM[0])
+    settle(PAD + 8, nxl - 16, FM[1, 8:nxl - 8] + RM[1, 8:nxl - 8])
+    for side in range(2):
+        strips[side].wait_recv()
+        begin = PAD - 8 if side == 0 else PAD + nxl - 8
+        wide = slice(begin, begin + 16)
+        FX[wide] = G[0, wide] * (1.0 / levels_total) * (FE[side, 0] + RE[side, 0])
+        inward = slice(8, 16) if side == 0 else slice(0, 8)
+        settle(PAD if side == 0 else PAD + nxl - 8, 8, FE[side, 1, inward] + RE[side, 1, inward])
+
+    for side, group in ((0, leftward), (1, rightward)):
+        @pl.when(have[side])
+        def _():
+            for copy in (*group[0], *group[1], *corners[side]):
+                copy.wait_send()
+
+    for copy in (planes, weights, inner, *strips):
+        copy.wait_send()
+
+
 def write(nxl, held, fresh, weight, flow_out, new_thickness, overburden, done):
     copies = [
         pltpu.make_async_copy(held.at[:, :, pl.ds(PAD, nxl)], flow_out, done.at[0]),
@@ -404,20 +790,31 @@
         rows = nxl + 2 * PAD
         f32 = jnp.float32
         vmem = pl.BlockSpec(memory_space=pltpu.VMEM)
-        held, fresh, weight = pl.pallas_call(
-            functools.partial(kernel, nx, nz, nl, nxl),
-            out_shape=(
-                pltpu.VMEM((4, nl, rows, ny), f32),
-                pltpu.VMEM(thickness.shape, f32),
-                pltpu.VMEM(density.shape, f32),
-            ),
-            in_specs=[pl.BlockSpec(memory_space=pl.ANY)] * 7,
-            out_specs=(vmem, vmem, vmem),
-            scratch_shapes=[
-                pltpu.VMEM((5, depth, rows, ny), f32),
-                pltpu.VMEM((4, depth, rows, ny), f32),
-                pltpu.VMEM((6, depth, rows, ny), f32),
-                pltpu.VMEM((2, depth, rows, ny), f32),
+        block = [pltpu.VMEM((n, depth, rows, ny), f32) for n in (5, 4, 6, 2)]
+        if nz == 2 and nx % 2 == 0 and nl > ZH and nxl >= 24:
+            body_of = functools.partial(paired, nx, nl, nxl)
+            scratch = block + [
+                pltpu.VMEM((3, rows, ny), f32),
+                pltpu.VMEM((nxl, ny), jnp.int32),
+                pltpu.VMEM((2, 8, ny), f32),
+                pltpu.VMEM((2, 8, ny), f32),
+                pltpu.VMEM((nxl, ny), f32),
+                pltpu.VMEM((nl, nxl, ny), f32),
+                pltpu.VMEM((4, rows, ny), f32),
+                pltpu.VMEM((rows, ny), f32),
+                pltpu.VMEM((2, nxl, ny), f32),
+                pltpu.VMEM((2, nxl, ny), f32),
+                pltpu.VMEM((2, 2, 16, ny), f32),
+                pltpu.VMEM((2, 2, 16, ny), f32),
+                pltpu.VMEM((nxl, ny), f32),
+                pltpu.VMEM((nxl, ny), f32),
+                pltpu.SemaphoreType.DMA((7,)),
+                pltpu.SemaphoreType.DMA((19,)),
+                pltpu.SemaphoreType.DMA((19,)),
+            ]
+        else:
+            body_of = functools.partial(kernel, nx, nz, nl, nxl)
+            scratch = block + [
                 pltpu.VMEM((2, rows, ny), f32),
                 pltpu.VMEM((rows, ny), jnp.int32),
                 pltpu.VMEM((nxl, ny), f32),
@@ -431,7 +828,17 @@
                 pltpu.SemaphoreType.DMA((12,)),
                 pltpu.SemaphoreType.DMA((nz - 1,)),
                 pltpu.SemaphoreType.DMA((nz - 1,)),
-            ],
+            ]
+        held, fresh, weight = pl.pallas_call(
+            body_of,
+            out_shape=(
+                pltpu.VMEM((4, nl, rows, ny), f32),
+                pltpu.VMEM(thickness.shape, f32),
+                pltpu.VMEM(density.shape, f32),
+            ),
+            in_specs=[pl.BlockSpec(memory_space=pl.ANY)] * 7,
+            out_specs=(vmem, vmem, vmem),
+            scratch_shapes=scratch,
             compiler_params=pltpu.CompilerParams(collective_id=0, has_side_effects=True),
         )(flow, fluid, density, thickness, bed, smb, mask)
         anywhere = pl.BlockSpec(memory_space=pl.ANY)

time: 13.6 us -> 12.7 us (0.934)
  Pallas kernels: 12.8 us -> 11.8 us
    pallas_call x1, Pallas kernels: 11.9 us -> 11 us  [body(): pl.pallas_call(body_of, out_shape=(pltpu.VMEM((4, nl, rows, ny), f32), pl...]
where the time goes in v2:
time: 12.7 us; the launch traced here: 12.5 us
  Pallas kernels  11.8 us (93%)
  between operations  0.64 us (5%)
    pallas_call x1, Pallas kernels, body(): pl.pallas_call(body_of, out_shape=(pltpu.VMEM((4, nl, rows, ny), f32), pl...  11 us
    pallas_call x1, Pallas kernels, body(): pl.pallas_call(functools.partial(write, nxl), out_shape=(jax.ShapeDtypeSt...  0.86 us

profile of v2, /device:TPU:29, one launch (start us, length us, event | category | flops | bytes accessed | tf_op | source)
XLA Modules:
  0.0 12.5 jit_solution(13416118364495164399)
XLA Ops:
  0.6 11.0 %shard_map.94 = (f32[4,8,64,128]{3,2,1,0:T(8,128)S(1)}, f32[32,128]{1,0:T(8,128)S(1)}, f32[8,32,128]{2,1,0:T(8,128)S(1)}) custom-call(f32[4,8,32,128]{3,2,1,0:T(8,128)} %flow.1, f32[8,32,128]{2,1,0:T(8,128)} %fluid.1, f32[8,32,128]{2,1,0:T(8,128)} %density.1, f32[32,128]{1,0:T(8,128)} %thickness.1, f32[32,128]{1,0:T(8,128)} %bed.1, f32[32,128]{1,0:T(8,128)} %smb.1, ...), custom_call_target="tpu_custom_call" | custom-call | tf_op jit(solution)/shard_map/pallas_call | solution.py:832
  11.6 0.9 %shard_map.95 = (f32[4,8,32,128]{3,2,1,0:T(8,128)}, f32[32,128]{1,0:T(8,128)}, f32[8,32,128]{2,1,0:T(8,128)}) custom-call(f32[4,8,64,128]{3,2,1,0:T(8,128)S(1)} %get-tuple-element.6.held, f32[32,128]{1,0:T(8,128)S(1)} %get-tuple-element.7.fresh, f32[8,32,128]{2,1,0:T(8,128)S(1)} %get-tuple-element.8.weight), custom_call_target="tpu_custom_call" | custom-call | tf_op jit(solution)/shard_map/pallas_call | solution.py:845

commit v3 on v2

--- a/solution.py
+++ b/solution.py
@@ -521,11 +521,11 @@
     planes.start()
 
     launch(rightward[0], (odd == 1) & has_right)
-    launch(leftward[0], (odd == 0) & has_left)
+    launch(leftward[0], (odd == 0) & has_left & jnp.logical_not(eager))
     launch(leftward[1], (odd == 1) & jnp.logical_not(eager))
     launch(rightward[1], (odd == 0) & jnp.logical_not(eager))
     launch(rightward[1], (odd == 1) & has_right)
-    launch(leftward[1], (odd == 0) & has_left)
+    launch(leftward[1], (odd == 0) & has_left & jnp.logical_not(eager))
 
 
     def dy(f):
@@ -642,6 +642,8 @@
     weights.start()
 
     apart(2, 2, move_first, middle)
+    launch(leftward[0], (odd == 0) & has_left & eager)
+    launch(leftward[1], (odd == 0) & has_left & eager)
     apart(1, 2, stress_last, middle)
     apart(0, 2, move_last, middle)
     planes.wait_recv()
@@ -655,9 +657,7 @@
             for copy in corners[side]:
                 copy.start()
 
-    place = lax.rem(gx, 4)
-    crossed = ((place == 2) & (gx > 2)) | ((place == 1) & (gx > 1) & (gx < nx - 3))
-    left_leads = (gx == 0) | (((odd == 1) != crossed) & has_right)
+    left_leads = (gx == 0) | ((odd == 1) & has_right)
 
     def by_arrival(step):
         @pl.when(left_leads)
@@ -751,13 +751,19 @@
     inner.wait_recv()
     FX[mine] = G[0, mine] * (1.0 / levels_total) * (FM[0] + RM[0])
     settle(PAD + 8, nxl - 16, FM[1, 8:nxl - 8] + RM[1, 8:nxl - 8])
-    for side in range(2):
+    def conclude(side):
         strips[side].wait_recv()
         begin = PAD - 8 if side == 0 else PAD + nxl - 8
         wide = slice(begin, begin + 16)
         FX[wide] = G[0, wide] * (1.0 / levels_total) * (FE[side, 0] + RE[side, 0])
         inward = slice(8, 16) if side == 0 else slice(0, 8)
         settle(PAD if side == 0 else PAD + nxl - 8, 8, FE[side, 1, inward] + RE[side, 1, inward])
+
+    def close(lead, other):
+        conclude(lead)
+        conclude(other)
+
+    by_arrival(close)
 
     for side, group in ((0, leftward), (1, rightward)):
         @pl.when(have[side])

time: 12.7 us -> 12.6 us (level)
  no operation moved by 1% of the time
where the time goes in v3:
time: 12.6 us; the launch traced here: 12.5 us
  Pallas kernels  11.8 us (94%)
  between operations  0.64 us (5%)
    pallas_call x1, Pallas kernels, body(): pl.pallas_call(body_of, out_shape=(pltpu.VMEM((4, nl, rows, ny), f32), pl...  11 us
    pallas_call x1, Pallas kernels, body(): pl.pallas_call(functools.partial(write, nxl), out_shape=(jax.ShapeDtypeSt...  0.86 us

profile of v3, /device:TPU:29, one launch (start us, length us, event | category | flops | bytes accessed | tf_op | source)
XLA Modules:
  0.0 12.5 jit_solution(11228690405434614344)
XLA Ops:
  0.6 11.0 %shard_map.94 = (f32[4,8,64,128]{3,2,1,0:T(8,128)S(1)}, f32[32,128]{1,0:T(8,128)S(1)}, f32[8,32,128]{2,1,0:T(8,128)S(1)}) custom-call(f32[4,8,32,128]{3,2,1,0:T(8,128)} %flow.1, f32[8,32,128]{2,1,0:T(8,128)} %fluid.1, f32[8,32,128]{2,1,0:T(8,128)} %density.1, f32[32,128]{1,0:T(8,128)} %thickness.1, f32[32,128]{1,0:T(8,128)} %bed.1, f32[32,128]{1,0:T(8,128)} %smb.1, ...), custom_call_target="tpu_custom_call" | custom-call | tf_op jit(solution)/shard_map/pallas_call | solution.py:838
  11.6 0.9 %shard_map.95 = (f32[4,8,32,128]{3,2,1,0:T(8,128)}, f32[32,128]{1,0:T(8,128)}, f32[8,32,128]{2,1,0:T(8,128)}) custom-call(f32[4,8,64,128]{3,2,1,0:T(8,128)S(1)} %get-tuple-element.6.held, f32[32,128]{1,0:T(8,128)S(1)} %get-tuple-element.7.fresh, f32[8,32,128]{2,1,0:T(8,128)S(1)} %get-tuple-element.8.weight), custom_call_target="tpu_custom_call" | custom-call | tf_op jit(solution)/shard_map/pallas_call | solution.py:851

commit v4 on v3

--- a/solution.py
+++ b/solution.py
@@ -642,9 +642,9 @@
     weights.start()
 
     apart(2, 2, move_first, middle)
+    apart(1, 2, stress_last, middle)
     launch(leftward[0], (odd == 0) & has_left & eager)
     launch(leftward[1], (odd == 0) & has_left & eager)
-    apart(1, 2, stress_last, middle)
     apart(0, 2, move_last, middle)
     planes.wait_recv()
     facing_part(3, 2, stress_first, middle)
@@ -717,8 +717,8 @@
             for copy in incoming[side][1]:
                 copy.wait_recv()
 
-        rest(3, 5, stress_first, area)
-        rest(2, 6, move_first, shifted)
+        rest(3, 3, stress_first, area)
+        rest(2, 3, move_first, shifted)
         rest(1, 4, stress_last, area)
         rest(0, 4, move_last, area)
         wide = slice(PAD - 8, PAD + 8) if side == 0 else slice(PAD + nxl - 8, PAD + nxl + 8)

time: 12.6 us -> 12.6 us (level)
  no operation moved by 1% of the time
where the time goes in v4:
time: 12.6 us; the launch traced here: 12.5 us
  Pallas kernels  11.8 us (94%)
  between operations  0.64 us (5%)
    pallas_call x1, Pallas kernels, body(): pl.pallas_call(body_of, out_shape=(pltpu.VMEM((4, nl, rows, ny), f32), pl...  10.9 us
    pallas_call x1, Pallas kernels, body(): pl.pallas_call(functools.partial(write, nxl), out_shape=(jax.ShapeDtypeSt...  0.86 us

profile of v4, /device:TPU:29, one launch (start us, length us, event | category | flops | bytes accessed | tf_op | source)
XLA Modules:
  0.0 12.5 jit_solution(4671799134727162491)
XLA Ops:
  0.6 10.9 %shard_map.94 = (f32[4,8,64,128]{3,2,1,0:T(8,128)S(1)}, f32[32,128]{1,0:T(8,128)S(1)}, f32[8,32,128]{2,1,0:T(8,128)S(1)}) custom-call(f32[4,8,32,128]{3,2,1,0:T(8,128)} %flow.1, f32[8,32,128]{2,1,0:T(8,128)} %fluid.1, f32[8,32,128]{2,1,0:T(8,128)} %density.1, f32[32,128]{1,0:T(8,128)} %thickness.1, f32[32,128]{1,0:T(8,128)} %bed.1, f32[32,128]{1,0:T(8,128)} %smb.1, ...), custom_call_target="tpu_custom_call" | custom-call | tf_op jit(solution)/shard_map/pallas_call | solution.py:838
  11.6 0.9 %shard_map.95 = (f32[4,8,32,128]{3,2,1,0:T(8,128)}, f32[32,128]{1,0:T(8,128)}, f32[8,32,128]{2,1,0:T(8,128)}) custom-call(f32[4,8,64,128]{3,2,1,0:T(8,128)S(1)} %get-tuple-element.6.held, f32[32,128]{1,0:T(8,128)S(1)} %get-tuple-element.7.fresh, f32[8,32,128]{2,1,0:T(8,128)S(1)} %get-tuple-element.8.weight), custom_call_target="tpu_custom_call" | custom-call | tf_op jit(solution)/shard_map/pallas_call | solution.py:851
